TPU v7x, 128 devices: a whole 4x4x4 slice. The times are simulated.
128 devices in a mesh: seq: 16 (over x_lo, y, core), hid: 8 (over x_hi, z).
Axes of the slice: x: 4 (x_hi: 2, x_lo: 2; x = x_hi * 2 + x_lo), y: 4, z: 4, core: 2. Of those that a mesh axis runs over, the one named last changes fastest.
Arguments:
- hidden: bfloat16 [8192, 4096], P('seq', 'hid'), may hold values from -6 to 6
- w_in: bfloat16 [2, 4096, 1024], P(None, 'hid'), may hold values from -0.09863281 to 0.09863281
- embedding: bfloat16 [1, 2048, 1024], replicated, may hold values from -6 to 6
- depth_gain: float32 [2, 1024], replicated, may hold values from 0.25 to 1.75
- w_out: bfloat16 [1024, 2, 2048], P(('seq', 'hid')), may hold values from -0.43554688 to 0.43554688
- codebook_ids: int32 [2, 8192], P(None, ('seq', 'hid')), may hold values from 0 to 2047
Outputs:
- grad_hidden: bfloat16 [8192, 4096], P('seq', 'hid')
- grad_in: float32 [2, 4096, 1024], P(None, 'hid', 'seq')
- grad_out: float32 [1024, 2, 2048], P(('seq', 'hid'))
All inputs are finite; a program needn't handle non-finite values.
Results may differ from a plain program's by a relative error of at most 0.01.
Values may be sent and summed in bfloat16 or wider, within the bound.
A program may use at most 128 MiB of HBM per device.

v0:
```python
import jax
import jax.numpy as jnp
from jax import lax
from jax.sharding import PartitionSpec as P


def shards(hidden, w_in, embedding, depth_gain, w_out, codebook_ids):
    hid_count = lax.axis_size("hid")
    seq_count = lax.axis_size("seq")
    width_in = hidden.shape[1] * hid_count
    steps = w_in.shape[0]
    depth = w_in.shape[2]
    entries = w_out.shape[2]
    group_rows = hidden.shape[0]
    hidden_f = hidden.astype(jnp.float32)
    square_part = jnp.sum(hidden_f * hidden_f, axis=1)
    proj_part = jnp.einsum("fd,kde->fke", hidden, w_in, preferred_element_type=jnp.float32)
    proj_flat, squares = (
        lax.psum_scatter(
            proj_part.reshape(group_rows, steps * depth), "hid", scatter_dimension=0, tiled=True
        ),
        lax.psum_scatter(square_part, "hid", scatter_dimension=0, tiled=True),
    )
    owned = proj_flat.shape[0]
    proj = proj_flat.reshape(owned, steps, depth)
    ratio = lax.rsqrt(squares / width_in + 1e-06)
    pieces = [jnp.zeros((owned, depth), jnp.float32)]
    pieces.append(jnp.take(embedding[0], codebook_ids[0], axis=0).astype(jnp.float32))
    x_rows = ratio[:, None, None] * proj + jnp.stack(pieces, axis=1)
    scale = lax.rsqrt(jnp.mean(x_rows * x_rows, axis=2, keepdims=True) + 1e-06)
    normed = (x_rows * scale * depth_gain[None]).astype(jnp.bfloat16)
    full_head = lax.all_gather(w_out, ("seq", "hid"), axis=0, tiled=True)
    logits = jnp.einsum("fkd,dkc->fkc", normed, full_head, preferred_element_type=jnp.float32)
    targets = codebook_ids.T
    lse = jax.nn.logsumexp(logits, axis=2)
    onehot = (targets[:, :, None] == jnp.arange(entries, dtype=jnp.int32)[None, None, :]).astype(
        jnp.float32
    )
    loss_weight = 2.0 * entries / (owned * seq_count * hid_count)
    d_logit = ((jnp.exp(logits - lse[:, :, None]) - onehot) * loss_weight).astype(jnp.bfloat16)
    grad_out = lax.psum_scatter(
        jnp.einsum("fkd,fkc->dkc", normed, d_logit, preferred_element_type=jnp.float32),
        ("seq", "hid"),
        scatter_dimension=0,
        tiled=True,
    )
    d_norm = jnp.einsum("fkc,dkc->fkd", d_logit, full_head, preferred_element_type=jnp.float32)
    gated = depth_gain[None] * d_norm
    d_x = scale * gated - x_rows * scale**3 * jnp.mean(gated * x_rows, axis=2, keepdims=True)
    d_round = d_x.astype(jnp.bfloat16)
    d_ratio = jnp.sum(d_x * proj, axis=(1, 2))
    correction = ratio**3 * d_ratio / width_in
    rows_back, ratio_back, corr_back = (
        lax.all_gather(d_round, "hid", axis=0, tiled=True),
        lax.all_gather(ratio.astype(jnp.bfloat16), "hid", axis=0, tiled=True).astype(ratio.dtype),
        lax.all_gather(correction.astype(jnp.bfloat16), "hid", axis=0, tiled=True).astype(
            correction.dtype
        ),
    )
    scaled = (ratio_back[:, None, None] * rows_back.astype(jnp.float32)).astype(jnp.bfloat16)
    in_term = jnp.einsum("fd,fke->kde", hidden, scaled, preferred_element_type=jnp.float32)
    grad_in = lax.psum_scatter(in_term, "seq", scatter_dimension=2, tiled=True)
    back = jnp.einsum("fke,kde->fd", rows_back, w_in, preferred_element_type=jnp.float32)
    grad_hidden = (ratio_back[:, None] * back - corr_back[:, None] * hidden_f).astype(jnp.bfloat16)
    return (grad_hidden, grad_in, grad_out)


def solution(mesh):
    placed = (
        P("seq", "hid"),
        P(None, "hid", None),
        P(),
        P(),
        P(("seq", "hid"), None, None),
        P(None, ("seq", "hid")),
    )
    return jax.shard_map(
        shards,
        mesh=mesh,
        in_specs=placed,
        out_specs=(P("seq", "hid"), P(None, "hid", "seq"), P(("seq", "hid"), None, None)),
        check_vma=False,
    )
```

profile of v0, /device:TPU:1, one launch (start us, length us, event | category | flops | bytes accessed | tf_op | source)
XLA Modules:
  0.0 623.6 jit_solution(17267702258610093383)
XLA Ops:
  8.1 1.5 copy-done
  9.6 4.3 fusion.7
  13.9 5.4 copy.31
  19.4 0.7 copy-done.5
  20.1 0.7 copy.22
  20.9 0.6 fusion.16
  22.2 3.5 gather_fusion
  25.9 23.2 %all-reduce.3 = f32[512]{0:T(512)S(1)} all-reduce(f32[512]{0:T(512)S(1)} %fusion.5), channel_id=2, replica_groups=mesh['seq'=16,'hid'=8] {'hid'}, use_global_device_ids=true, to_apply=%region_1.0.clone | all-reduce | flops 512 | bytes 4096
  49.2 58.5 %reduce-scatter.7.cloned.1.call-done = f32[64,2048]{1,0:T(8,128)} async-done(((f32[512,2048]{1,0:T(8,128)}), f32[64,2048]{1,0:T(8,128)}) %reduce-scatter.7.cloned.1.call-update) | async-done | bytes 524304
  107.7 2.4 copy.32
  110.1 1.5 copy.21
  111.9 236.0 %all-gather.3.cloned.1.call-done = bf16[1024,2,2048]{2,0,1:T(8,128)(2,1)} async-done(((bf16[8,2,2048]{2,0,1:T(8,128)(2,1)}), bf16[1024,2,2048]{2,0,1:T(8,128)(2,1)}) %all-gather.3.cloned.1.call-update) | async-done | bytes 8388624 | tf_op jit(solution)/shard_map/all_gather | solution.py:32
  347.9 5.3 fusion.17
  353.2 0.3 exponential_reduce_fusion
  353.7 2.8 multiply_reduce_fusion.1
  356.5 1.0 multiply_reduce_fusion
  357.6 9.4 %convolution_bitcast_fusion = f32[1024,2,2048]{0,2,1:T(8,128)} fusion(f32[2,1024]{1,0:T(2,128)S(1)} %copy-done.4, f32[64,2]{0,1:T(2,128)S(1)} %get-tuple-element.16, f32[64,2,2048]{2,0,1:T(8,128)} %copy-done.2, s32[64,2]{0,1:T(2,128)S(1)} %bitcast.45, f32[64,2]{0,1:T(2,128)S(1)} %log_add_fusion, f32[64,2,1024]{2,0,1:T(8,128)S(1)} %copy.21, ...), kind=kOutput, calls=%fused_computation.1 | convolution fusion | flops 539230208 | bytes 18491136 | tf_op jit(solution)/shard_map/fkd,fkc->dkc/dot_general | solution.py:42
  367.0 25.4 %copy.25 = f32[1024,2,2048]{2,1,0:T(2,128)} copy(f32[1024,2,2048]{0,2,1:T(8,128)} %convolution_bitcast_fusion) | data formatting | bytes 33554432 | tf_op jit(solution)/shard_map/fkd,fkc->dkc/transpose | solution.py:42
  393.1 0.2 dynamic-update-slice
  393.6 21.0 %all-reduce.5 = (bf16[512]{0:T(512)(128)(2,1)S(1)}, bf16[512]{0:T(512)(128)(2,1)S(1)}) all-reduce(bf16[512]{0:T(512)(128)(2,1)S(1)} %dynamic-update-slice.1, bf16[512]{0:T(512)(128)(2,1)S(1)} %dynamic-update-slice), channel_id=1, replica_groups=mesh['seq'=16,'hid'=8] {'hid'}, use_global_device_ids=true, to_apply=%add.2 | all-reduce | flops 1024 | bytes 4096
  414.7 5.2 convolution_bitcast_fusion.2
  419.9 3.8 fusion.3
  423.6 191.3 %all-reduce.8.cloned.1.call-done = f32[1024,2,2048]{2,1,0:T(2,128)} async-done(((f32[1024,2,2048]{2,1,0:T(2,128)}), f32[1024,2,2048]{2,1,0:T(2,128)}) %all-reduce.8.cloned.1.call-update) | async-done | bytes 16777232
  615.0 1.6 constant_dynamic-slice_fusion
  (43 shorter events, 1.4 us)
Async XLA Ops:
  8.0 1.6 copy-start
  8.0 99.7 %reduce-scatter.7.cloned.1.call-start = ((), (), s32[]{:S(2)}) async-start(), calls=%async_computation.5 | async-start | bytes 4718592
  19.3 0.8 copy-start.5
  19.3 1.6 copy-start.7
  19.3 2.8 copy-start.6
  19.3 6.4 %copy-start.3 = (bf16[512,512]{1,0:T(8,128)(2,1)S(1)}, bf16[512,512]{1,0:T(8,128)(2,1)}, u32[]{:S(2)}) copy-start(bf16[512,512]{1,0:T(8,128)(2,1)} %param.6) | copy-start | bytes 1572868
  19.3 328.6 %copy-start.4 = (f32[2,1024]{1,0:T(2,128)S(1)}, f32[2,1024]{1,0:T(2,128)}, u32[]{:S(2)}) copy-start(f32[2,1024]{1,0:T(2,128)} %param.9) | copy-start | bytes 24580
  19.3 328.5 %all-gather.3.cloned.1.call-start = ((), (), s32[]{:S(2)}) async-start(), calls=%async_computation.2 | async-start | bytes 8454144 | tf_op jit(solution)/shard_map/all_gather | solution.py:32
  20.8 393.8 %all-gather.5.cloned.1.call-start = ((), (), s32[]{:S(2)}) async-start(), calls=%async_computation.3 | async-start | bytes 2359296 | tf_op jit(solution)/shard_map/all_gather | solution.py:54
  347.9 5.8 copy-start.1
  353.2 3.3 copy-start.2
  357.5 257.4 %all-reduce.8.cloned.1.call-start = ((), (), s32[]{:S(2)}) async-start(), calls=%async_computation.6 | async-start | bytes 33554432
  392.4 224.1 %reduce-scatter.5.cloned.1.call-start = ((), (), s32[]{:S(2)}) async-start(), calls=%async_computation.4 | async-start | bytes 4456448 | tf_op jit(solution)/shard_map/reduce_scatter | solution.py:62
Sparse Core Ops, SparseCore 0:
  19.5 88.1 reduce-scatter.6
  357.6 55.4 all-gather.4
  420.0 69.6 reduce-scatter.4
Sparse Core Ops, SparseCore 1:
  22.1 325.7 all-gather.2
  392.5 222.4 all-reduce.7
where the time goes:
time: 625 us; the launch traced here: 624 us
  waiting for transfers between devices  486 us (78%)
  local copies, waits for them, and re-layouts  44.2 us (7%)
  blocking collectives  44.1 us (7%)
  matrix products  30.7 us (5%)
  between operations  16.6 us (3%)
    unnamed x7, waiting for transfers between devices  250 us
    all_gather x1, waiting for transfers between devices, shards(): full_head = lax.all_gather(w_out, ('seq', 'hid'), axis=0, tiled=True)  236 us
    unnamed x2, blocking collectives  44.1 us
    transpose x1, local copies, waits for them, and re-layouts, shards(): jnp.einsum('fkd,fkc->dkc', normed, d_logit, preferred_element_type=jnp.fl...  25.4 us
    unnamed x25, local copies, waits for them, and re-layouts  13.7 us
  transfers between devices with their start and end apart: 5, of which 3 were waited for; matrix products, arithmetic and copies ran while one was open for 9% of the time, Pallas kernels for 0%

commit v1 on v0

--- a/solution.py
+++ b/solution.py
@@ -29,7 +29,8 @@
     x_rows = ratio[:, None, None] * proj + jnp.stack(pieces, axis=1)
     scale = lax.rsqrt(jnp.mean(x_rows * x_rows, axis=2, keepdims=True) + 1e-06)
     normed = (x_rows * scale * depth_gain[None]).astype(jnp.bfloat16)
-    full_head = lax.all_gather(w_out, ("seq", "hid"), axis=0, tiled=True)
+    repeated = jnp.stack([w_out] * lax.axis_size(("seq", "hid")))
+    full_head = jnp.concatenate(lax.all_to_all(repeated, ("seq", "hid"), 0, 0), axis=0)
     logits = jnp.einsum("fkd,dkc->fkc", normed, full_head, preferred_element_type=jnp.float32)
     targets = codebook_ids.T
     lse = jax.nn.logsumexp(logits, axis=2)

time: 625 us -> 560 us (0.90)
  waiting for transfers between devices: 486 us -> 321 us
  blocking collectives: 44.1 us -> 126 us
  starting transfers between devices: 0.21 us -> 12.1 us
    all_gather x1 -> x0, waiting for transfers between devices: 236 us -> none  [shards(): full_head = lax.all_gather(w_out, ('seq', 'hid'), axis=0, tiled=True)]
    unnamed x2, blocking collectives: 44.1 us -> 126 us
    reduce_scatter x1, waiting for transfers between devices: 0.01 us -> 63.2 us  [shards(): grad_in = lax.psum_scatter(in_term, 'seq', scatter_dimension=2, tiled=True)]
    all_to_all x0 -> x1, starting transfers between devices: none -> 11.9 us  [shards(): lax.all_to_all(repeated, ('seq', 'hid'), 0, 0)]
    unnamed x7 -> x6, waiting for transfers between devices: 250 us -> 258 us
    unnamed x25 -> x23, local copies, waits for them, and re-layouts: 13.7 us -> 12.8 us
  transfers between devices with their start and end apart: 5 -> 5, of which waited for: 3 -> 3; matrix products, arithmetic and copies ran while one was open for 9% -> 11% of each run, Pallas kernels for 0% -> 0%
where the time goes in v1:
time: 560 us; the launch traced here: 556 us
  waiting for transfers between devices  321 us (57%)
  blocking collectives  126 us (22%)
  local copies, waits for them, and re-layouts  47.6 us (8%)
  matrix products  32.9 us (6%)
  between operations  15.2 us (3%)
  starting transfers between devices  12.1 us (2%)
    unnamed x6, waiting for transfers between devices  258 us
    unnamed x2, blocking collectives  126 us
    reduce_scatter x1, waiting for transfers between devices, shards(): grad_in = lax.psum_scatter(in_term, 'seq', scatter_dimension=2, tiled=True)  63.2 us
    transpose x1, local copies, waits for them, and re-layouts, shards(): jnp.einsum('fkd,fkc->dkc', normed, d_logit, preferred_element_type=jnp.fl...  25.4 us
    unnamed x23, local copies, waits for them, and re-layouts  12.8 us
    all_to_all x1, starting transfers between devices, shards(): lax.all_to_all(repeated, ('seq', 'hid'), 0, 0)  11.9 us
  transfers between devices with their start and end apart: 5, of which 3 were waited for; matrix products, arithmetic and copies ran while one was open for 11% of the time, Pallas kernels for 0%

profile of v1, /device:TPU:1, one launch (start us, length us, event | category | flops | bytes accessed | tf_op | source)
XLA Modules:
  0.0 556.1 jit_solution(9693335959632997892)
XLA Ops:
  7.2 1.5 copy-done
  8.8 4.3 fusion.21
  13.0 5.4 copy.32
  18.4 0.8 copy-done.3
  19.3 4.3 stack.8
  23.5 11.9 %all-to-all-start = ((bf16[128,8,2,2048]{3,1,2,0:T(8,128)(2,1)}), bf16[128,8,2,2048]{3,1,2,0:T(8,128)(2,1)}, u32[]{:S(2)}, u32[]{:S(2)}) async-start(bf16[128,8,2,2048]{3,1,2,0:T(8,128)(2,1)} %stack.8), calls=%async_computation | async-start | bytes 16777216 | tf_op jit(solution)/shard_map/all_to_all | solution.py:33
  35.6 0.6 fusion.30
  36.9 3.5 gather_fusion
  40.6 107.6 %all-reduce.3 = f32[512]{0:T(512)S(1)} all-reduce(f32[512]{0:T(512)S(1)} %fusion.19), channel_id=2, replica_groups=mesh['seq'=16,'hid'=8] {'hid'}, use_global_device_ids=true, to_apply=%region_1.0.clone | all-reduce | flops 512 | bytes 4096
  148.4 47.2 %reduce-scatter.7.cloned.1.call-done = f32[64,2048]{1,0:T(8,128)} async-done(((f32[512,2048]{1,0:T(8,128)}), f32[64,2048]{1,0:T(8,128)}) %reduce-scatter.7.cloned.1.call-update) | async-done | bytes 524304
  195.5 2.4 copy.33
  197.9 1.5 copy.21
  199.7 5.1 fusion.31
  204.9 0.3 exponential_reduce_fusion
  205.2 5.2 multiply_reduce_fusion.1
  210.4 1.0 multiply_reduce_fusion
  211.5 9.4 %convolution_bitcast_fusion = f32[1024,2,2048]{0,2,1:T(8,128)} fusion(f32[2,1024]{1,0:T(2,128)S(1)} %copy-done.4, f32[64,2]{0,1:T(2,128)S(1)} %get-tuple-element.16, f32[64,2,2048]{2,0,1:T(8,128)} %copy-done.2, s32[64,2]{0,1:T(2,128)S(1)} %bitcast.58, f32[64,2]{0,1:T(2,128)S(1)} %log_add_fusion, f32[64,2,1024]{2,0,1:T(8,128)S(1)} %copy.21, ...), kind=kOutput, calls=%fused_computation.7 | convolution fusion | flops 539230208 | bytes 18491136 | tf_op jit(solution)/shard_map/fkd,fkc->dkc/dot_general | solution.py:43
  220.9 25.4 %copy.26 = f32[1024,2,2048]{2,1,0:T(2,128)} copy(f32[1024,2,2048]{0,2,1:T(8,128)} %convolution_bitcast_fusion) | data formatting | bytes 33554432 | tf_op jit(solution)/shard_map/fkd,fkc->dkc/transpose | solution.py:43
  247.6 18.0 %all-reduce.5 = (bf16[512]{0:T(512)(128)(2,1)S(1)}, bf16[512]{0:T(512)(128)(2,1)S(1)}) all-reduce(bf16[512]{0:T(512)(128)(2,1)S(1)} %dynamic-update-slice.1, bf16[512]{0:T(512)(128)(2,1)S(1)} %dynamic-update-slice), channel_id=1, replica_groups=mesh['seq'=16,'hid'=8] {'hid'}, use_global_device_ids=true, to_apply=%add.2 | all-reduce | flops 1024 | bytes 4096
  265.6 5.2 convolution_bitcast_fusion.1
  270.8 3.7 fusion.12
  274.5 210.4 %all-reduce.8.cloned.1.call-done = f32[1024,2,2048]{2,1,0:T(2,128)} async-done(((f32[1024,2,2048]{2,1,0:T(2,128)}), f32[1024,2,2048]{2,1,0:T(2,128)}) %all-reduce.8.cloned.1.call-update) | async-done | bytes 16777232
  484.8 1.6 constant_dynamic-slice_fusion
  486.4 63.2 %reduce-scatter.5.cloned.1.call-done = f32[2,512,64]{1,2,0:T(8,128)} async-done(((f32[2,512,1024]{1,2,0:T(8,128)}), f32[2,512,64]{1,2,0:T(8,128)}) %reduce-scatter.5.cloned.1.call-update) | async-done | bytes 262160 | tf_op jit(solution)/shard_map/reduce_scatter | solution.py:63
  (41 shorter events, 1.4 us)
Async XLA Ops:
  7.2 1.6 copy-start
  7.2 188.4 %reduce-scatter.7.cloned.1.call-start = ((), (), s32[]{:S(2)}) async-start(), calls=%async_computation.5 | async-start | bytes 4718592
  18.4 0.8 copy-start.3
  23.5 12.0 %copy-start.6 = (u32[128]{0:T(128)S(1)}, u32[128]{0:T(128)}, u32[]{:S(2)}) copy-start(u32[128]{0:T(128)} %constant.44) | copy-start | bytes 1540
  23.5 13.3 %copy-start.5 = (s32[2,64]{1,0:T(2,128)S(1)}, s32[2,64]{1,0:T(2,128)}, u32[]{:S(2)}) copy-start(s32[2,64]{1,0:T(2,128)} %param.11) | copy-start | bytes 1540
  23.5 16.9 %copy-start.1 = (bf16[512,512]{1,0:T(8,128)(2,1)S(1)}, bf16[512,512]{1,0:T(8,128)(2,1)}, u32[]{:S(2)}) copy-start(bf16[512,512]{1,0:T(8,128)(2,1)} %param.6) | copy-start | bytes 1572868
  23.5 176.2 %all-to-all-start = ((bf16[128,8,2,2048]{3,1,2,0:T(8,128)(2,1)}), bf16[128,8,2,2048]{3,1,2,0:T(8,128)(2,1)}, u32[]{:S(2)}, u32[]{:S(2)}) async-start(bf16[128,8,2,2048]{3,1,2,0:T(8,128)(2,1)} %stack.8), calls=%async_computation | async-start | bytes 16777216 | tf_op jit(solution)/shard_map/all_to_all | solution.py:33
  35.5 164.2 %copy-start.4 = (f32[2,1024]{1,0:T(2,128)S(1)}, f32[2,1024]{1,0:T(2,128)}, u32[]{:S(2)}) copy-start(f32[2,1024]{1,0:T(2,128)} %param.9) | copy-start | bytes 24580
  35.5 230.1 %all-gather.2.cloned.1.call-start = ((), (), s32[]{:S(2)}) async-start(), calls=%async_computation.3 | async-start | bytes 2359296 | tf_op jit(solution)/shard_map/all_gather | solution.py:55
  204.8 5.6 %copy-start.2 = (f32[64,2,2048]{2,0,1:T(8,128)}, f32[64,2,2048]{2,0,1:T(8,128)S(1)}, u32[]{:S(2)}) copy-start(f32[64,2,2048]{2,0,1:T(8,128)S(1)} %get-tuple-element.20) | copy-start | bytes 3145732
  211.5 273.4 %all-reduce.8.cloned.1.call-start = ((), (), s32[]{:S(2)}) async-start(), calls=%async_computation.6 | async-start | bytes 33554432
  246.4 303.2 %reduce-scatter.5.cloned.1.call-start = ((), (), s32[]{:S(2)}) async-start(), calls=%async_computation.4 | async-start | bytes 4456448 | tf_op jit(solution)/shard_map/reduce_scatter | solution.py:63
Sparse Core Ops, SparseCore 0:
  18.5 176.9 reduce-scatter.6
  211.6 53.2 all-gather.1
  270.4 214.3 all-reduce.7
  487.7 61.8 reduce-scatter.4
